TPU v7x, 128 devices: a whole 4x4x4 slice. The times are simulated.
128 devices in a mesh: gx: 4 (over z_lo, core), gy: 4 (over y), gz: 8 (over x, z_hi).
Axes of the slice: x: 4, y: 4, z: 4 (z_hi: 2, z_lo: 2; z = z_hi * 2 + z_lo), core: 2. Of those that a mesh axis runs over, the one named last changes fastest.
Arguments:
- gradients: bfloat16 [128, 3072, 512], P(('gx', 'gy', 'gz')), may hold values from -24 to 24
- master_weights: float32 [3072, 512], P(('gx', 'gy', 'gz')), may hold values from -10 to 10
- first_moment: float32 [3072, 512], P(('gx', 'gy', 'gz')), may hold values from -8 to 8
- second_moment: float32 [3072, 512], P(('gx', 'gy', 'gz')), may hold values from 1 to 100
- tensor_ids: int32 [3072], P(('gx', 'gy', 'gz')), may hold values from 0 to 3, as said below
Outputs:
- new_master: float32 [3072, 512], P(('gx', 'gy', 'gz'))
- new_first: float32 [3072, 512], P(('gx', 'gy', 'gz'))
- new_second: float32 [3072, 512], P(('gx', 'gy', 'gz'))
- scaled_update: float32 [3072, 512], P(('gx', 'gy', 'gz'))
- params: bfloat16 [3072, 512], replicated
Inputs may be any that keep to these rules, and one draw needn't show every extreme that they name: `tensor_ids`: nondecreasing along the rows; every tensor of 4 owns one contiguous run of rows.
All inputs are finite; a program needn't handle non-finite values.
Results may differ from a plain program's by a relative error of at most 0.0045.
Values may be sent and summed in bfloat16 or wider, within the bound.
No kernel may reach another device: no remote copies, remote signals or barrier semaphores. Data moves between devices by JAX's collectives and lax.ppermute only.
A program may use at most 64 MiB of HBM per device.

v0:
```python
import functools
import jax
import jax.numpy as jnp
from jax import lax
from jax.sharding import Mesh
from jax.sharding import PartitionSpec as P

NT = 4
GX = ("gx_0", "gx_1")
GZ = ("gz_0", "gz_1")
GX_GY_GZ = ("gx_0", "gx_1", "gy", "gz_0", "gz_1")
decay_first = 0.9
decay_second = 0.999
epsilon = 1e-06
weight_decay = 0.01
step_size = 0.05


def split_up(value, dim, length):
    before, after = (value.shape[:dim], value.shape[dim + 1 :])
    return jnp.moveaxis(value.reshape(*before, length, -1, *after), dim, 0)


def sum_at_owner(value, axis, dim):
    blocks = split_up(value, dim, lax.axis_size(axis))
    arrived = lax.all_to_all(blocks, axis, split_axis=0, concat_axis=0, tiled=True)
    return arrived.astype(jnp.float32).sum(axis=0)


def one_axis_at_a_time(value, axes):
    return functools.reduce(lax.psum, axes, value)


def copy_for_each(value, axis):
    length = lax.axis_size(axis)
    return lax.all_to_all(
        jnp.broadcast_to(value[None], (length, *value.shape)), axis, 0, 0, tiled=True
    )


def laid_out(blocks, dim):
    lengths = list(blocks.shape[1:])
    lengths[dim] *= blocks.shape[0]
    return jnp.moveaxis(blocks, 0, dim).reshape(lengths)


def gather_directly(value, axis, dim):
    blocks = copy_for_each(value, axis)
    return laid_out(blocks, dim)


def tensor_sums(values, onehot):
    return jnp.dot(jnp.sum(values * values, axis=1), onehot, precision=lax.Precision.HIGHEST)


def on_device(gradients, master_weights, first_moment, second_moment, tensor_ids):
    count_across = lax.axis_size(GX)
    count_down = lax.axis_size("gy")
    count_along = lax.axis_size(GZ)
    own_rows, row_width = master_weights.shape
    own_gradient = gradients[0].astype(jnp.float32)
    onehot = (tensor_ids[:, None] == jnp.arange(NT, dtype=jnp.int32)[None, :]).astype(jnp.float32)
    counts = jnp.sum(onehot, axis=0) * row_width
    weight_local = tensor_sums(master_weights, onehot)
    blocks = own_gradient.reshape(count_across, count_down, count_along, own_rows, row_width)
    third_rows = own_rows // 3
    first_part = blocks[:, :, :, :third_rows]
    first_part = sum_at_owner(first_part.astype(jnp.bfloat16), GX, 0)
    first_part = sum_at_owner(first_part.astype(jnp.bfloat16), "gy", 1)
    first_part = sum_at_owner(first_part.astype(jnp.bfloat16), GZ, 2)
    second_part = blocks[:, :, :, third_rows : 2 * third_rows]
    second_part = sum_at_owner(second_part.astype(jnp.bfloat16), "gy", 1)
    second_part = sum_at_owner(second_part.astype(jnp.bfloat16), GZ, 2)
    second_part = sum_at_owner(second_part.astype(jnp.bfloat16), GX, 0)
    third_part = blocks[:, :, :, 2 * third_rows :]
    third_part = sum_at_owner(third_part.astype(jnp.bfloat16), GZ, 2)
    third_part = sum_at_owner(third_part.astype(jnp.bfloat16), GX, 0)
    third_part = sum_at_owner(third_part.astype(jnp.bfloat16), "gy", 1)
    summed = jnp.concatenate((first_part, second_part, third_part), axis=3).reshape(
        own_rows, row_width
    )
    new_first = decay_first * first_moment + (1.0 - decay_first) * summed
    new_second = decay_second * second_moment + (1.0 - decay_second) * summed * summed
    update = new_first / (jnp.sqrt(new_second) + epsilon) + weight_decay * master_weights
    update_local = tensor_sums(update, onehot)
    weight_sq, update_sq, total_counts = (
        one_axis_at_a_time(weight_local, GX_GY_GZ),
        one_axis_at_a_time(update_local, GX_GY_GZ),
        one_axis_at_a_time(counts, GX_GY_GZ),
    )
    trust_ratio = jnp.sqrt(weight_sq / (update_sq + total_counts))
    row_trust = jnp.dot(onehot, trust_ratio, precision=lax.Precision.HIGHEST)
    scaled_update = row_trust[:, None] * update
    new_master = master_weights - step_size * scaled_update
    params = new_master.astype(jnp.bfloat16)
    stacked = params.reshape(1, 1, 1, own_rows, row_width)
    stacked = gather_directly(stacked, GZ, 2)
    stacked = gather_directly(stacked, "gy", 1)
    stacked = lax.all_gather(stacked, GX, axis=0, tiled=True)
    gathered = stacked.reshape(count_across * count_down * count_along * own_rows, row_width)
    return (new_master, new_first, new_second, scaled_update, gathered)


def solution(mesh):
    torus = Mesh(
        mesh.devices.reshape(2, 2, mesh.shape["gy"], 4, 2), ("gx_0", "gx_1", "gy", "gz_0", "gz_1")
    )
    return jax.shard_map(
        on_device,
        mesh=torus,
        in_specs=(
            P(GX_GY_GZ, None, None),
            P(GX_GY_GZ, None),
            P(GX_GY_GZ, None),
            P(GX_GY_GZ, None),
            P(GX_GY_GZ),
        ),
        out_specs=(P(GX_GY_GZ, None), P(GX_GY_GZ, None), P(GX_GY_GZ, None), P(GX_GY_GZ, None), P()),
        check_vma=False,
    )
```

profile of v0, /device:TPU:1, one launch (start us, length us, event | category | flops | bytes accessed | tf_op | source)
XLA Modules:
  0.0 229.2 jit_solution(9659133965096885783)
XLA Ops:
  7.2 3.1 %slice_bitcast_fusion.2 = (bf16[4,1,4,8,8,512]{5,4,3,2,1,0:T(8,128)(2,1)}, bf16[8,4,4,1,8,512]{5,4,0,2,1,3:T(8,128)(2,1)S(1)}, bf16[4,4,1,8,8,512]{5,4,3,0,1,2:T(8,128)(2,1)S(1)}) fusion(bf16[4,4,8,24,512]{4,3,2,1,0:T(8,128)(2,1)} %bitcast.49), kind=kLoop, calls=%fused_computation.6 | loop fusion | bytes 6291456 | tf_op jit(solution)/shard_map/reshape | solution.py:21
  10.3 4.9 %all-to-all-start = ((bf16[4,1,4,8,8,512]{5,4,3,2,1,0:T(8,128)(2,1)}), bf16[4,1,4,8,8,512]{5,4,3,2,1,0:T(8,128)(2,1)S(1)}, u32[]{:S(2)}, u32[]{:S(2)}) async-start(bf16[4,1,4,8,8,512]{5,4,3,2,1,0:T(8,128)(2,1)} %get-tuple-element.22), calls=%async_computation | async-start | bytes 2097152 | tf_op jit(solution)/shard_map/all_to_all | solution.py:26
  15.2 1.1 copy.15
  16.2 12.4 %all-to-all-done = bf16[4,1,4,8,8,512]{5,4,3,2,1,0:T(8,128)(2,1)S(1)} async-done(((bf16[4,1,4,8,8,512]{5,4,3,2,1,0:T(8,128)(2,1)}), bf16[4,1,4,8,8,512]{5,4,3,2,1,0:T(8,128)(2,1)S(1)}, u32[]{:S(2)}, u32[]{:S(2)}) %all-to-all-start) | async-done | bytes 1048608 | tf_op jit(solution)/shard_map/all_to_all | solution.py:26
  28.6 4.3 %all-to-all-start.3 = ((bf16[4,4,1,8,8,512]{5,4,3,1,2,0:T(8,128)(2,1)}), bf16[4,4,1,8,8,512]{5,4,3,1,2,0:T(8,128)(2,1)S(1)}, u32[]{:S(2)}, u32[]{:S(2)}) async-start(bf16[4,4,1,8,8,512]{5,4,3,1,2,0:T(8,128)(2,1)} %copy.15), calls=%async_computation.3 | async-start | bytes 2097152 | tf_op jit(solution)/shard_map/all_to_all | solution.py:26
  32.9 1.1 copy.17
  34.0 12.8 %all-to-all-done.3 = bf16[4,4,1,8,8,512]{5,4,3,1,2,0:T(8,128)(2,1)S(1)} async-done(((bf16[4,4,1,8,8,512]{5,4,3,1,2,0:T(8,128)(2,1)}), bf16[4,4,1,8,8,512]{5,4,3,1,2,0:T(8,128)(2,1)S(1)}, u32[]{:S(2)}, u32[]{:S(2)}) %all-to-all-start.3) | async-done | bytes 1048608 | tf_op jit(solution)/shard_map/all_to_all | solution.py:26
  46.9 7.3 %all-to-all-start.6 = ((bf16[8,4,4,1,8,512]{5,4,2,1,3,0:T(8,128)(2,1)}), bf16[8,4,4,1,8,512]{5,4,2,1,3,0:T(8,128)(2,1)S(1)}, u32[]{:S(2)}, u32[]{:S(2)}) async-start(bf16[8,4,4,1,8,512]{5,4,2,1,3,0:T(8,128)(2,1)} %copy.17), calls=%async_computation.6 | async-start | bytes 2097152 | tf_op jit(solution)/shard_map/all_to_all | solution.py:26
  54.2 0.9 reduce_sum.133
  55.1 13.5 %all-to-all-done.6 = bf16[8,4,4,1,8,512]{5,4,2,1,3,0:T(8,128)(2,1)S(1)} async-done(((bf16[8,4,4,1,8,512]{5,4,2,1,3,0:T(8,128)(2,1)}), bf16[8,4,4,1,8,512]{5,4,2,1,3,0:T(8,128)(2,1)S(1)}, u32[]{:S(2)}, u32[]{:S(2)}) %all-to-all-start.6) | async-done | bytes 1048608 | tf_op jit(solution)/shard_map/all_to_all | solution.py:26
  68.6 3.4 %all-to-all-start.1 = ((bf16[4,1,1,8,8,512]{5,4,3,2,1,0:T(8,128)(2,1)}), bf16[4,1,1,8,8,512]{5,4,3,2,1,0:T(8,128)(2,1)S(1)}, u32[]{:S(2)}, u32[]{:S(2)}) async-start(bf16[4,1,1,8,8,512]{5,4,3,2,1,0:T(8,128)(2,1)} %bitcast.4), calls=%async_computation.1 | async-start | bytes 524288 | tf_op jit(solution)/shard_map/all_to_all | solution.py:26
  72.0 0.8 reduce_sum.141
  72.9 4.7 %all-to-all-done.1 = bf16[4,1,1,8,8,512]{5,4,3,2,1,0:T(8,128)(2,1)S(1)} async-done(((bf16[4,1,1,8,8,512]{5,4,3,2,1,0:T(8,128)(2,1)}), bf16[4,1,1,8,8,512]{5,4,3,2,1,0:T(8,128)(2,1)S(1)}, u32[]{:S(2)}, u32[]{:S(2)}) %all-to-all-start.1) | async-done | bytes 262176 | tf_op jit(solution)/shard_map/all_to_all | solution.py:26
  77.5 7.2 %all-to-all-start.7 = ((bf16[4,1,4,1,8,512]{5,4,2,3,1,0:T(8,128)(2,1)}), bf16[4,1,4,1,8,512]{5,4,2,3,1,0:T(8,128)(2,1)S(1)}, u32[]{:S(2)}, u32[]{:S(2)}) async-start(bf16[4,1,4,1,8,512]{5,4,2,3,1,0:T(8,128)(2,1)} %bitcast.15), calls=%async_computation.7 | async-start | bytes 262144 | tf_op jit(solution)/shard_map/all_to_all | solution.py:26
  85.7 2.6 %all-to-all-done.7 = bf16[4,1,4,1,8,512]{5,4,2,3,1,0:T(8,128)(2,1)S(1)} async-done(((bf16[4,1,4,1,8,512]{5,4,2,3,1,0:T(8,128)(2,1)}), bf16[4,1,4,1,8,512]{5,4,2,3,1,0:T(8,128)(2,1)S(1)}, u32[]{:S(2)}, u32[]{:S(2)}) %all-to-all-start.7) | async-done | bytes 131104 | tf_op jit(solution)/shard_map/all_to_all | solution.py:26
  88.3 3.5 %all-to-all-start.4 = ((bf16[8,4,1,1,8,512]{5,4,1,3,2,0:T(8,128)(2,1)}), bf16[8,4,1,1,8,512]{5,4,1,3,2,0:T(8,128)(2,1)S(1)}, u32[]{:S(2)}, u32[]{:S(2)}) async-start(bf16[8,4,1,1,8,512]{5,4,1,3,2,0:T(8,128)(2,1)} %copy.16), calls=%async_computation.4 | async-start | bytes 524288 | tf_op jit(solution)/shard_map/all_to_all | solution.py:26
  92.5 6.6 %all-to-all-done.4 = bf16[8,4,1,1,8,512]{5,4,1,3,2,0:T(8,128)(2,1)S(1)} async-done(((bf16[8,4,1,1,8,512]{5,4,1,3,2,0:T(8,128)(2,1)}), bf16[8,4,1,1,8,512]{5,4,1,3,2,0:T(8,128)(2,1)S(1)}, u32[]{:S(2)}, u32[]{:S(2)}) %all-to-all-start.4) | async-done | bytes 262176 | tf_op jit(solution)/shard_map/all_to_all | solution.py:26
  99.1 3.3 %all-to-all-start.2 = ((bf16[8,1,1,1,8,512]{5,4,3,2,1,0:T(8,128)(2,1)}), bf16[8,1,1,1,8,512]{5,4,3,2,1,0:T(8,128)(2,1)S(1)}, u32[]{:S(2)}, u32[]{:S(2)}) async-start(bf16[8,1,1,1,8,512]{5,4,3,2,1,0:T(8,128)(2,1)} %bitcast.5), calls=%async_computation.2 | async-start | bytes 131072 | tf_op jit(solution)/shard_map/all_to_all | solution.py:26
  103.9 5.1 %all-to-all-done.2 = bf16[8,1,1,1,8,512]{5,4,3,2,1,0:T(8,128)(2,1)S(1)} async-done(((bf16[8,1,1,1,8,512]{5,4,3,2,1,0:T(8,128)(2,1)}), bf16[8,1,1,1,8,512]{5,4,3,2,1,0:T(8,128)(2,1)S(1)}, u32[]{:S(2)}, u32[]{:S(2)}) %all-to-all-start.2) | async-done | bytes 65568 | tf_op jit(solution)/shard_map/all_to_all | solution.py:26
  109.0 3.3 %all-to-all-start.8 = ((bf16[4,1,1,1,8,512]{5,4,3,2,1,0:T(8,128)(2,1)}), bf16[4,1,1,1,8,512]{5,4,3,2,1,0:T(8,128)(2,1)S(1)}, u32[]{:S(2)}, u32[]{:S(2)}) async-start(bf16[4,1,1,1,8,512]{5,4,3,2,1,0:T(8,128)(2,1)} %bitcast.16), calls=%async_computation.8 | async-start | bytes 65536 | tf_op jit(solution)/shard_map/all_to_all | solution.py:26
  112.3 4.2 %all-to-all-done.8 = bf16[4,1,1,1,8,512]{5,4,3,2,1,0:T(8,128)(2,1)S(1)} async-done(((bf16[4,1,1,1,8,512]{5,4,3,2,1,0:T(8,128)(2,1)}), bf16[4,1,1,1,8,512]{5,4,3,2,1,0:T(8,128)(2,1)S(1)}, u32[]{:S(2)}, u32[]{:S(2)}) %all-to-all-start.8) | async-done | bytes 32800 | tf_op jit(solution)/shard_map/all_to_all | solution.py:26
  116.6 8.0 %all-to-all-start.5 = ((bf16[4,1,1,1,8,512]{5,4,3,2,1,0:T(8,128)(2,1)}), bf16[4,1,1,1,8,512]{5,4,3,2,1,0:T(8,128)(2,1)S(1)}, u32[]{:S(2)}, u32[]{:S(2)}) async-start(bf16[4,1,1,1,8,512]{5,4,3,2,1,0:T(8,128)(2,1)} %bitcast.11), calls=%async_computation.5 | async-start | bytes 65536 | tf_op jit(solution)/shard_map/all_to_all | solution.py:26
  124.6 3.2 %all-to-all-done.5 = bf16[4,1,1,1,8,512]{5,4,3,2,1,0:T(8,128)(2,1)S(1)} async-done(((bf16[4,1,1,1,8,512]{5,4,3,2,1,0:T(8,128)(2,1)}), bf16[4,1,1,1,8,512]{5,4,3,2,1,0:T(8,128)(2,1)S(1)}, u32[]{:S(2)}, u32[]{:S(2)}) %all-to-all-start.5) | async-done | bytes 32800 | tf_op jit(solution)/shard_map/all_to_all | solution.py:26
  128.8 3.8 %all-reduce.4 = (f32[4]{0:T(128)S(1)}, f32[4]{0:T(128)S(1)}) all-reduce(f32[4]{0:T(128)S(1)} %convolution_bitcast_fusion.2, f32[4]{0:T(128)S(1)} %fusion), channel_id=1, replica_groups=mesh['gx_0'=2,'gx_1'=2,'gy'=4,'gz_0'=4,'gz_1'=2] {'gx_0'}, use_global_device_ids=true, to_apply=%region_1.0 | all-reduce | flops 8 | bytes 64 | tf_op jit(solution)/shard_map/psum | solution.py:31
  132.6 4.0 %all-reduce.3 = (f32[4]{0:T(128)S(1)}, f32[4]{0:T(128)S(1)}) all-reduce(f32[4]{0:T(128)S(1)} %get-tuple-element.13, f32[4]{0:T(128)S(1)} %get-tuple-element.14), channel_id=1, replica_groups=mesh['gx_0'=2,'gx_1'=2,'gy'=4,'gz_0'=4,'gz_1'=2] {'gx_1'}, use_global_device_ids=true, to_apply=%region_2.0 | all-reduce | flops 8 | bytes 64 | tf_op jit(solution)/shard_map/psum | solution.py:31
  136.6 6.8 %all-reduce.1 = (f32[4]{0:T(128)S(1)}, f32[4]{0:T(128)S(1)}) all-reduce(f32[4]{0:T(128)S(1)} %get-tuple-element.11, f32[4]{0:T(128)S(1)} %get-tuple-element.12), channel_id=1, replica_groups=mesh['gx_0'=2,'gx_1'=2,'gy'=4,'gz_0'=4,'gz_1'=2] {'gy'}, use_global_device_ids=true, to_apply=%region_3.0 | all-reduce | flops 8 | bytes 64 | tf_op jit(solution)/shard_map/psum | solution.py:31
  143.4 6.9 %all-reduce = (f32[4]{0:T(128)S(1)}, f32[4]{0:T(128)S(1)}) all-reduce(f32[4]{0:T(128)S(1)} %get-tuple-element.7, f32[4]{0:T(128)S(1)} %get-tuple-element.8), channel_id=1, replica_groups=mesh['gx_0'=2,'gx_1'=2,'gy'=4,'gz_0'=4,'gz_1'=2] {'gz_0'}, use_global_device_ids=true, to_apply=%region_4.0 | all-reduce | flops 8 | bytes 64 | tf_op jit(solution)/shard_map/psum | solution.py:31
  150.3 5.3 %all-reduce.2 = (f32[4]{0:T(128)S(1)}, f32[4]{0:T(128)S(1)}) all-reduce(f32[4]{0:T(128)S(1)} %get-tuple-element.5, f32[4]{0:T(128)S(1)} %get-tuple-element.6), channel_id=1, replica_groups=mesh['gx_0'=2,'gx_1'=2,'gy'=4,'gz_0'=4,'gz_1'=2] {'gz_1'}, use_global_device_ids=true, to_apply=%region_5.0 | all-reduce | flops 8 | bytes 64 | tf_op jit(solution)/shard_map/psum | solution.py:31
  156.4 9.4 %all_to_all.55 = bf16[8,1,1,1,24,512]{5,4,3,2,1,0:T(8,128)(2,1)S(1)} all-to-all(bf16[8,1,1,1,24,512]{5,4,3,2,1,0:T(8,128)(2,1)S(1)} %broadcast_in_dim.6), channel_id=1, replica_groups=mesh['gx_0'=2,'gx_1'=2,'gy'=4,'gz_0'=4,'gz_1'=2] {'gz_0','gz_1'}, dimensions={0} | all-to-all | bytes 393216 | tf_op jit(solution)/shard_map/all_to_all | solution.py:36
  165.9 11.5 %all_to_all.56 = bf16[4,1,1,8,24,512]{5,4,3,2,1,0:T(8,128)(2,1)} all-to-all(bf16[4,1,1,8,24,512]{5,4,3,2,1,0:T(8,128)(2,1)S(1)} %broadcast_in_dim.8), channel_id=1, replica_groups=mesh['gx_0'=2,'gx_1'=2,'gy'=4,'gz_0'=4,'gz_1'=2] {'gy'}, dimensions={0} | all-to-all | bytes 1572864 | tf_op jit(solution)/shard_map/all_to_all | solution.py:36
  177.4 41.2 %all-gather.3.cloned.1.call-done = bf16[16,1,1,8,24,512]{5,4,3,2,1,0:T(8,128)(2,1)} async-done(((bf16[4,1,1,8,24,512]{5,4,3,2,1,0:T(8,128)(2,1)}), bf16[16,1,1,8,24,512]{5,4,3,2,1,0:T(8,128)(2,1)}) %all-gather.3.cloned.1.call-update) | async-done | bytes 3145744 | tf_op jit(solution)/shard_map/all_gather | solution.py:99
  218.6 3.8 %copy.19 = bf16[3072,512]{1,0:T(8,128)(2,1)} copy(bf16[3072,512]{1,0:T(8,128)(2,1)} %bitcast.50) | data formatting | bytes 6291456
  (26 shorter events, 5.0 us)
Async XLA Ops:
  10.3 18.3 %all-to-all-start = ((bf16[4,1,4,8,8,512]{5,4,3,2,1,0:T(8,128)(2,1)}), bf16[4,1,4,8,8,512]{5,4,3,2,1,0:T(8,128)(2,1)S(1)}, u32[]{:S(2)}, u32[]{:S(2)}) async-start(bf16[4,1,4,8,8,512]{5,4,3,2,1,0:T(8,128)(2,1)} %get-tuple-element.22), calls=%async_computation | async-start | bytes 2097152 | tf_op jit(solution)/shard_map/all_to_all | solution.py:26
  28.6 18.3 %all-to-all-start.3 = ((bf16[4,4,1,8,8,512]{5,4,3,1,2,0:T(8,128)(2,1)}), bf16[4,4,1,8,8,512]{5,4,3,1,2,0:T(8,128)(2,1)S(1)}, u32[]{:S(2)}, u32[]{:S(2)}) async-start(bf16[4,4,1,8,8,512]{5,4,3,1,2,0:T(8,128)(2,1)} %copy.15), calls=%async_computation.3 | async-start | bytes 2097152 | tf_op jit(solution)/shard_map/all_to_all | solution.py:26
  46.9 21.8 %all-to-all-start.6 = ((bf16[8,4,4,1,8,512]{5,4,2,1,3,0:T(8,128)(2,1)}), bf16[8,4,4,1,8,512]{5,4,2,1,3,0:T(8,128)(2,1)S(1)}, u32[]{:S(2)}, u32[]{:S(2)}) async-start(bf16[8,4,4,1,8,512]{5,4,2,1,3,0:T(8,128)(2,1)} %copy.17), calls=%async_computation.6 | async-start | bytes 2097152 | tf_op jit(solution)/shard_map/all_to_all | solution.py:26
  54.2 48.3 %copy-start.3 = (s32[24]{0:T(128)S(1)}, s32[24]{0:T(128)}, u32[]{:S(2)}) copy-start(s32[24]{0:T(128)} %param.9) | copy-start | bytes 292
  54.2 73.5 %copy-start = (f32[24,512]{1,0:T(8,128)S(1)}, f32[24,512]{1,0:T(8,128)}, u32[]{:S(2)}) copy-start(f32[24,512]{1,0:T(8,128)} %param.6) | copy-start | bytes 147460
  54.2 73.5 %copy-start.1 = (f32[24,512]{1,0:T(8,128)S(1)}, f32[24,512]{1,0:T(8,128)}, u32[]{:S(2)}) copy-start(f32[24,512]{1,0:T(8,128)} %param.8) | copy-start | bytes 147460
  54.2 73.5 %copy-start.2 = (f32[24,512]{1,0:T(8,128)S(1)}, f32[24,512]{1,0:T(8,128)}, u32[]{:S(2)}) copy-start(f32[24,512]{1,0:T(8,128)} %param.7) | copy-start | bytes 147460
  68.6 8.9 %all-to-all-start.1 = ((bf16[4,1,1,8,8,512]{5,4,3,2,1,0:T(8,128)(2,1)}), bf16[4,1,1,8,8,512]{5,4,3,2,1,0:T(8,128)(2,1)S(1)}, u32[]{:S(2)}, u32[]{:S(2)}) async-start(bf16[4,1,1,8,8,512]{5,4,3,2,1,0:T(8,128)(2,1)} %bitcast.4), calls=%async_computation.1 | async-start | bytes 524288 | tf_op jit(solution)/shard_map/all_to_all | solution.py:26
  77.5 10.8 %all-to-all-start.7 = ((bf16[4,1,4,1,8,512]{5,4,2,3,1,0:T(8,128)(2,1)}), bf16[4,1,4,1,8,512]{5,4,2,3,1,0:T(8,128)(2,1)S(1)}, u32[]{:S(2)}, u32[]{:S(2)}) async-start(bf16[4,1,4,1,8,512]{5,4,2,3,1,0:T(8,128)(2,1)} %bitcast.15), calls=%async_computation.7 | async-start | bytes 262144 | tf_op jit(solution)/shard_map/all_to_all | solution.py:26
  88.3 10.8 %all-to-all-start.4 = ((bf16[8,4,1,1,8,512]{5,4,1,3,2,0:T(8,128)(2,1)}), bf16[8,4,1,1,8,512]{5,4,1,3,2,0:T(8,128)(2,1)S(1)}, u32[]{:S(2)}, u32[]{:S(2)}) async-start(bf16[8,4,1,1,8,512]{5,4,1,3,2,0:T(8,128)(2,1)} %copy.16), calls=%async_computation.4 | async-start | bytes 524288 | tf_op jit(solution)/shard_map/all_to_all | solution.py:26
  99.1 9.9 %all-to-all-start.2 = ((bf16[8,1,1,1,8,512]{5,4,3,2,1,0:T(8,128)(2,1)}), bf16[8,1,1,1,8,512]{5,4,3,2,1,0:T(8,128)(2,1)S(1)}, u32[]{:S(2)}, u32[]{:S(2)}) async-start(bf16[8,1,1,1,8,512]{5,4,3,2,1,0:T(8,128)(2,1)} %bitcast.5), calls=%async_computation.2 | async-start | bytes 131072 | tf_op jit(solution)/shard_map/all_to_all | solution.py:26
  109.0 7.5 %all-to-all-start.8 = ((bf16[4,1,1,1,8,512]{5,4,3,2,1,0:T(8,128)(2,1)}), bf16[4,1,1,1,8,512]{5,4,3,2,1,0:T(8,128)(2,1)S(1)}, u32[]{:S(2)}, u32[]{:S(2)}) async-start(bf16[4,1,1,1,8,512]{5,4,3,2,1,0:T(8,128)(2,1)} %bitcast.16), calls=%async_computation.8 | async-start | bytes 65536 | tf_op jit(solution)/shard_map/all_to_all | solution.py:26
  116.6 11.2 %all-to-all-start.5 = ((bf16[4,1,1,1,8,512]{5,4,3,2,1,0:T(8,128)(2,1)}), bf16[4,1,1,1,8,512]{5,4,3,2,1,0:T(8,128)(2,1)S(1)}, u32[]{:S(2)}, u32[]{:S(2)}) async-start(bf16[4,1,1,1,8,512]{5,4,3,2,1,0:T(8,128)(2,1)} %bitcast.11), calls=%async_computation.5 | async-start | bytes 65536 | tf_op jit(solution)/shard_map/all_to_all | solution.py:26
  124.6 94.0 %all-gather.3.cloned.1.call-start = ((), (), s32[]{:S(2)}) async-start(), calls=%async_computation.11 | async-start | bytes 3932160 | tf_op jit(solution)/shard_map/all_gather | solution.py:99
Sparse Core Ops, SparseCore 0:
  177.5 40.9 all-gather.2
where the time goes:
time: 230 us; the launch traced here: 229 us
  waiting for transfers between devices  106 us (46%)
  blocking collectives  47.7 us (21%)
  starting transfers between devices  45.3 us (20%)
  between operations  14.1 us (6%)
  local copies, waits for them, and re-layouts  9.9 us (4%)
  other arithmetic  5.55 us (2%)
    all_to_all x9, waiting for transfers between devices, sum_at_owner(): lax.all_to_all(blocks, axis, split_axis=0, concat_axis=0, tiled=True)  65.1 us
    all_to_all x9, starting transfers between devices, sum_at_owner(): lax.all_to_all(blocks, axis, split_axis=0, concat_axis=0, tiled=True)  45.3 us
    all_gather x1, waiting for transfers between devices, on_device(): stacked = lax.all_gather(stacked, GX, axis=0, tiled=True)  41.2 us
    psum x5, blocking collectives, one_axis_at_a_time(): return functools.reduce(lax.psum, axes, value)  26.8 us
    all_to_all x2, blocking collectives, copy_for_each(): lax.all_to_all(jnp.broadcast_to(value[None], (length, *value.shape)), axi...  20.9 us
  transfers between devices with their start and end apart: 10, of which 10 were waited for; matrix products, arithmetic and copies ran while one was open for 3% of the time, Pallas kernels for 0%

commit v1 on v0

--- a/solution.py
+++ b/solution.py
@@ -96,7 +96,9 @@
     stacked = params.reshape(1, 1, 1, own_rows, row_width)
     stacked = gather_directly(stacked, GZ, 2)
     stacked = gather_directly(stacked, "gy", 1)
-    stacked = lax.all_gather(stacked, GX, axis=0, tiled=True)
+    stacked = jnp.concatenate(
+        lax.all_to_all(jnp.stack([stacked] * lax.axis_size(GX)), GX, 0, 0), axis=0
+    )
     gathered = stacked.reshape(count_across * count_down * count_along * own_rows, row_width)
     return (new_master, new_first, new_second, scaled_update, gathered)
 

time: 230 us -> 219 us (0.952)
  blocking collectives: 47.7 us -> 93.2 us
  waiting for transfers between devices: 106 us -> 65.1 us
  between operations: 14.1 us -> 0.77 us
    all_to_all x0 -> x1, blocking collectives: none -> 46.2 us  [on_device(): lax.all_to_all(jnp.stack([stacked] * lax.axis_size(GX)), GX, 0, 0)]
    all_gather x1 -> x0, waiting for transfers between devices: 41.2 us -> none  [on_device(): stacked = lax.all_gather(stacked, GX, axis=0, tiled=True)]
  transfers between devices with their start and end apart: 10 -> 9, of which waited for: 10 -> 9; matrix products, arithmetic and copies ran while one was open for 3% -> 3% of each run, Pallas kernels for 0% -> 0%
where the time goes in v1:
time: 219 us; the launch traced here: 218 us
  blocking collectives  93.2 us (43%)
  waiting for transfers between devices  65.1 us (30%)
  starting transfers between devices  45.3 us (21%)
  local copies, waits for them, and re-layouts  8.12 us (4%)
  other arithmetic  5.55 us (3%)
    all_to_all x9, waiting for transfers between devices, sum_at_owner(): lax.all_to_all(blocks, axis, split_axis=0, concat_axis=0, tiled=True)  65.1 us
    all_to_all x1, blocking collectives, on_device(): lax.all_to_all(jnp.stack([stacked] * lax.axis_size(GX)), GX, 0, 0)  46.2 us
    all_to_all x9, starting transfers between devices, sum_at_owner(): lax.all_to_all(blocks, axis, split_axis=0, concat_axis=0, tiled=True)  45.3 us
    psum x5, blocking collectives, one_axis_at_a_time(): return functools.reduce(lax.psum, axes, value)  26.8 us
    all_to_all x2, blocking collectives, copy_for_each(): lax.all_to_all(jnp.broadcast_to(value[None], (length, *value.shape)), axi...  20.2 us
  transfers between devices with their start and end apart: 9, of which 9 were waited for; matrix products, arithmetic and copies ran while one was open for 3% of the time, Pallas kernels for 0%

profile of v1, /device:TPU:1, one launch (start us, length us, event | category | flops | bytes accessed | tf_op | source)
XLA Modules:
  0.0 218.3 jit_solution(1322613680117789636)
XLA Ops:
  0.6 3.1 %slice_bitcast_fusion.2 = (bf16[4,1,4,8,8,512]{5,4,3,2,1,0:T(8,128)(2,1)}, bf16[8,4,4,1,8,512]{5,4,0,2,1,3:T(8,128)(2,1)S(1)}, bf16[4,4,1,8,8,512]{5,4,3,0,1,2:T(8,128)(2,1)S(1)}) fusion(bf16[4,4,8,24,512]{4,3,2,1,0:T(8,128)(2,1)} %bitcast.51), kind=kLoop, calls=%fused_computation.6 | loop fusion | bytes 6291456 | tf_op jit(solution)/shard_map/reshape | solution.py:21
  3.8 4.9 %all-to-all-start = ((bf16[4,1,4,8,8,512]{5,4,3,2,1,0:T(8,128)(2,1)}), bf16[4,1,4,8,8,512]{5,4,3,2,1,0:T(8,128)(2,1)S(1)}, u32[]{:S(2)}, u32[]{:S(2)}) async-start(bf16[4,1,4,8,8,512]{5,4,3,2,1,0:T(8,128)(2,1)} %get-tuple-element.22), calls=%async_computation | async-start | bytes 2097152 | tf_op jit(solution)/shard_map/all_to_all | solution.py:26
  8.6 1.1 copy.15
  9.7 12.4 %all-to-all-done = bf16[4,1,4,8,8,512]{5,4,3,2,1,0:T(8,128)(2,1)S(1)} async-done(((bf16[4,1,4,8,8,512]{5,4,3,2,1,0:T(8,128)(2,1)}), bf16[4,1,4,8,8,512]{5,4,3,2,1,0:T(8,128)(2,1)S(1)}, u32[]{:S(2)}, u32[]{:S(2)}) %all-to-all-start) | async-done | bytes 1048608 | tf_op jit(solution)/shard_map/all_to_all | solution.py:26
  22.1 4.3 %all-to-all-start.3 = ((bf16[4,4,1,8,8,512]{5,4,3,1,2,0:T(8,128)(2,1)}), bf16[4,4,1,8,8,512]{5,4,3,1,2,0:T(8,128)(2,1)S(1)}, u32[]{:S(2)}, u32[]{:S(2)}) async-start(bf16[4,4,1,8,8,512]{5,4,3,1,2,0:T(8,128)(2,1)} %copy.15), calls=%async_computation.3 | async-start | bytes 2097152 | tf_op jit(solution)/shard_map/all_to_all | solution.py:26
  26.4 1.1 copy.17
  27.5 12.8 %all-to-all-done.3 = bf16[4,4,1,8,8,512]{5,4,3,1,2,0:T(8,128)(2,1)S(1)} async-done(((bf16[4,4,1,8,8,512]{5,4,3,1,2,0:T(8,128)(2,1)}), bf16[4,4,1,8,8,512]{5,4,3,1,2,0:T(8,128)(2,1)S(1)}, u32[]{:S(2)}, u32[]{:S(2)}) %all-to-all-start.3) | async-done | bytes 1048608 | tf_op jit(solution)/shard_map/all_to_all | solution.py:26
  40.3 7.3 %all-to-all-start.6 = ((bf16[8,4,4,1,8,512]{5,4,2,1,3,0:T(8,128)(2,1)}), bf16[8,4,4,1,8,512]{5,4,2,1,3,0:T(8,128)(2,1)S(1)}, u32[]{:S(2)}, u32[]{:S(2)}) async-start(bf16[8,4,4,1,8,512]{5,4,2,1,3,0:T(8,128)(2,1)} %copy.17), calls=%async_computation.6 | async-start | bytes 2097152 | tf_op jit(solution)/shard_map/all_to_all | solution.py:26
  47.7 0.9 reduce_sum.133
  48.6 13.5 %all-to-all-done.6 = bf16[8,4,4,1,8,512]{5,4,2,1,3,0:T(8,128)(2,1)S(1)} async-done(((bf16[8,4,4,1,8,512]{5,4,2,1,3,0:T(8,128)(2,1)}), bf16[8,4,4,1,8,512]{5,4,2,1,3,0:T(8,128)(2,1)S(1)}, u32[]{:S(2)}, u32[]{:S(2)}) %all-to-all-start.6) | async-done | bytes 1048608 | tf_op jit(solution)/shard_map/all_to_all | solution.py:26
  62.1 3.4 %all-to-all-start.1 = ((bf16[4,1,1,8,8,512]{5,4,3,2,1,0:T(8,128)(2,1)}), bf16[4,1,1,8,8,512]{5,4,3,2,1,0:T(8,128)(2,1)S(1)}, u32[]{:S(2)}, u32[]{:S(2)}) async-start(bf16[4,1,1,8,8,512]{5,4,3,2,1,0:T(8,128)(2,1)} %bitcast.4), calls=%async_computation.1 | async-start | bytes 524288 | tf_op jit(solution)/shard_map/all_to_all | solution.py:26
  65.5 0.8 reduce_sum.141
  66.3 4.7 %all-to-all-done.1 = bf16[4,1,1,8,8,512]{5,4,3,2,1,0:T(8,128)(2,1)S(1)} async-done(((bf16[4,1,1,8,8,512]{5,4,3,2,1,0:T(8,128)(2,1)}), bf16[4,1,1,8,8,512]{5,4,3,2,1,0:T(8,128)(2,1)S(1)}, u32[]{:S(2)}, u32[]{:S(2)}) %all-to-all-start.1) | async-done | bytes 262176 | tf_op jit(solution)/shard_map/all_to_all | solution.py:26
  71.0 7.2 %all-to-all-start.7 = ((bf16[4,1,4,1,8,512]{5,4,2,3,1,0:T(8,128)(2,1)}), bf16[4,1,4,1,8,512]{5,4,2,3,1,0:T(8,128)(2,1)S(1)}, u32[]{:S(2)}, u32[]{:S(2)}) async-start(bf16[4,1,4,1,8,512]{5,4,2,3,1,0:T(8,128)(2,1)} %bitcast.15), calls=%async_computation.7 | async-start | bytes 262144 | tf_op jit(solution)/shard_map/all_to_all | solution.py:26
  79.1 2.6 %all-to-all-done.7 = bf16[4,1,4,1,8,512]{5,4,2,3,1,0:T(8,128)(2,1)S(1)} async-done(((bf16[4,1,4,1,8,512]{5,4,2,3,1,0:T(8,128)(2,1)}), bf16[4,1,4,1,8,512]{5,4,2,3,1,0:T(8,128)(2,1)S(1)}, u32[]{:S(2)}, u32[]{:S(2)}) %all-to-all-start.7) | async-done | bytes 131104 | tf_op jit(solution)/shard_map/all_to_all | solution.py:26
  81.8 3.5 %all-to-all-start.4 = ((bf16[8,4,1,1,8,512]{5,4,1,3,2,0:T(8,128)(2,1)}), bf16[8,4,1,1,8,512]{5,4,1,3,2,0:T(8,128)(2,1)S(1)}, u32[]{:S(2)}, u32[]{:S(2)}) async-start(bf16[8,4,1,1,8,512]{5,4,1,3,2,0:T(8,128)(2,1)} %copy.16), calls=%async_computation.4 | async-start | bytes 524288 | tf_op jit(solution)/shard_map/all_to_all | solution.py:26
  86.0 6.6 %all-to-all-done.4 = bf16[8,4,1,1,8,512]{5,4,1,3,2,0:T(8,128)(2,1)S(1)} async-done(((bf16[8,4,1,1,8,512]{5,4,1,3,2,0:T(8,128)(2,1)}), bf16[8,4,1,1,8,512]{5,4,1,3,2,0:T(8,128)(2,1)S(1)}, u32[]{:S(2)}, u32[]{:S(2)}) %all-to-all-start.4) | async-done | bytes 262176 | tf_op jit(solution)/shard_map/all_to_all | solution.py:26
  92.6 3.3 %all-to-all-start.2 = ((bf16[8,1,1,1,8,512]{5,4,3,2,1,0:T(8,128)(2,1)}), bf16[8,1,1,1,8,512]{5,4,3,2,1,0:T(8,128)(2,1)S(1)}, u32[]{:S(2)}, u32[]{:S(2)}) async-start(bf16[8,1,1,1,8,512]{5,4,3,2,1,0:T(8,128)(2,1)} %bitcast.5), calls=%async_computation.2 | async-start | bytes 131072 | tf_op jit(solution)/shard_map/all_to_all | solution.py:26
  97.4 5.1 %all-to-all-done.2 = bf16[8,1,1,1,8,512]{5,4,3,2,1,0:T(8,128)(2,1)S(1)} async-done(((bf16[8,1,1,1,8,512]{5,4,3,2,1,0:T(8,128)(2,1)}), bf16[8,1,1,1,8,512]{5,4,3,2,1,0:T(8,128)(2,1)S(1)}, u32[]{:S(2)}, u32[]{:S(2)}) %all-to-all-start.2) | async-done | bytes 65568 | tf_op jit(solution)/shard_map/all_to_all | solution.py:26
  102.5 3.3 %all-to-all-start.8 = ((bf16[4,1,1,1,8,512]{5,4,3,2,1,0:T(8,128)(2,1)}), bf16[4,1,1,1,8,512]{5,4,3,2,1,0:T(8,128)(2,1)S(1)}, u32[]{:S(2)}, u32[]{:S(2)}) async-start(bf16[4,1,1,1,8,512]{5,4,3,2,1,0:T(8,128)(2,1)} %bitcast.16), calls=%async_computation.8 | async-start | bytes 65536 | tf_op jit(solution)/shard_map/all_to_all | solution.py:26
  105.8 4.2 %all-to-all-done.8 = bf16[4,1,1,1,8,512]{5,4,3,2,1,0:T(8,128)(2,1)S(1)} async-done(((bf16[4,1,1,1,8,512]{5,4,3,2,1,0:T(8,128)(2,1)}), bf16[4,1,1,1,8,512]{5,4,3,2,1,0:T(8,128)(2,1)S(1)}, u32[]{:S(2)}, u32[]{:S(2)}) %all-to-all-start.8) | async-done | bytes 32800 | tf_op jit(solution)/shard_map/all_to_all | solution.py:26
  110.0 8.0 %all-to-all-start.5 = ((bf16[4,1,1,1,8,512]{5,4,3,2,1,0:T(8,128)(2,1)}), bf16[4,1,1,1,8,512]{5,4,3,2,1,0:T(8,128)(2,1)S(1)}, u32[]{:S(2)}, u32[]{:S(2)}) async-start(bf16[4,1,1,1,8,512]{5,4,3,2,1,0:T(8,128)(2,1)} %bitcast.11), calls=%async_computation.5 | async-start | bytes 65536 | tf_op jit(solution)/shard_map/all_to_all | solution.py:26
  118.0 3.2 %all-to-all-done.5 = bf16[4,1,1,1,8,512]{5,4,3,2,1,0:T(8,128)(2,1)S(1)} async-done(((bf16[4,1,1,1,8,512]{5,4,3,2,1,0:T(8,128)(2,1)}), bf16[4,1,1,1,8,512]{5,4,3,2,1,0:T(8,128)(2,1)S(1)}, u32[]{:S(2)}, u32[]{:S(2)}) %all-to-all-start.5) | async-done | bytes 32800 | tf_op jit(solution)/shard_map/all_to_all | solution.py:26
  122.3 3.8 %all-reduce.4 = (f32[4]{0:T(128)S(1)}, f32[4]{0:T(128)S(1)}) all-reduce(f32[4]{0:T(128)S(1)} %convolution_bitcast_fusion.2, f32[4]{0:T(128)S(1)} %fusion), channel_id=1, replica_groups=mesh['gx_0'=2,'gx_1'=2,'gy'=4,'gz_0'=4,'gz_1'=2] {'gx_0'}, use_global_device_ids=true, to_apply=%region_1.0 | all-reduce | flops 8 | bytes 64 | tf_op jit(solution)/shard_map/psum | solution.py:31
  126.0 4.0 %all-reduce.3 = (f32[4]{0:T(128)S(1)}, f32[4]{0:T(128)S(1)}) all-reduce(f32[4]{0:T(128)S(1)} %get-tuple-element.13, f32[4]{0:T(128)S(1)} %get-tuple-element.14), channel_id=1, replica_groups=mesh['gx_0'=2,'gx_1'=2,'gy'=4,'gz_0'=4,'gz_1'=2] {'gx_1'}, use_global_device_ids=true, to_apply=%region_2.0 | all-reduce | flops 8 | bytes 64 | tf_op jit(solution)/shard_map/psum | solution.py:31
  130.1 6.8 %all-reduce.1 = (f32[4]{0:T(128)S(1)}, f32[4]{0:T(128)S(1)}) all-reduce(f32[4]{0:T(128)S(1)} %get-tuple-element.11, f32[4]{0:T(128)S(1)} %get-tuple-element.12), channel_id=1, replica_groups=mesh['gx_0'=2,'gx_1'=2,'gy'=4,'gz_0'=4,'gz_1'=2] {'gy'}, use_global_device_ids=true, to_apply=%region_3.0 | all-reduce | flops 8 | bytes 64 | tf_op jit(solution)/shard_map/psum | solution.py:31
  136.9 6.9 %all-reduce = (f32[4]{0:T(128)S(1)}, f32[4]{0:T(128)S(1)}) all-reduce(f32[4]{0:T(128)S(1)} %get-tuple-element.7, f32[4]{0:T(128)S(1)} %get-tuple-element.8), channel_id=1, replica_groups=mesh['gx_0'=2,'gx_1'=2,'gy'=4,'gz_0'=4,'gz_1'=2] {'gz_0'}, use_global_device_ids=true, to_apply=%region_4.0 | all-reduce | flops 8 | bytes 64 | tf_op jit(solution)/shard_map/psum | solution.py:31
  143.8 5.3 %all-reduce.2 = (f32[4]{0:T(128)S(1)}, f32[4]{0:T(128)S(1)}) all-reduce(f32[4]{0:T(128)S(1)} %get-tuple-element.5, f32[4]{0:T(128)S(1)} %get-tuple-element.6), channel_id=1, replica_groups=mesh['gx_0'=2,'gx_1'=2,'gy'=4,'gz_0'=4,'gz_1'=2] {'gz_1'}, use_global_device_ids=true, to_apply=%region_5.0 | all-reduce | flops 8 | bytes 64 | tf_op jit(solution)/shard_map/psum | solution.py:31
  149.9 9.4 %all_to_all.60 = bf16[8,1,1,1,24,512]{5,4,3,2,1,0:T(8,128)(2,1)S(1)} all-to-all(bf16[8,1,1,1,24,512]{5,4,3,2,1,0:T(8,128)(2,1)S(1)} %broadcast_in_dim.6), channel_id=1, replica_groups=mesh['gx_0'=2,'gx_1'=2,'gy'=4,'gz_0'=4,'gz_1'=2] {'gz_0','gz_1'}, dimensions={0} | all-to-all | bytes 393216 | tf_op jit(solution)/shard_map/all_to_all | solution.py:36
  159.4 10.7 %all_to_all.61 = bf16[4,1,1,8,24,512]{5,4,3,2,1,0:T(8,128)(2,1)S(1)} all-to-all(bf16[4,1,1,8,24,512]{5,4,3,2,1,0:T(8,128)(2,1)S(1)} %broadcast_in_dim.8), channel_id=1, replica_groups=mesh['gx_0'=2,'gx_1'=2,'gy'=4,'gz_0'=4,'gz_1'=2] {'gy'}, dimensions={0} | all-to-all | bytes 1572864 | tf_op jit(solution)/shard_map/all_to_all | solution.py:36
  170.5 46.2 %all_to_all.62 = bf16[4,1,4,8,24,512]{5,4,3,2,1,0:T(8,128)(2,1)S(1)} all-to-all(bf16[4,1,4,8,24,512]{5,4,3,2,1,0:T(8,128)(2,1)S(1)} %stack.3), channel_id=1, replica_groups=mesh['gx_0'=2,'gx_1'=2,'gy'=4,'gz_0'=4,'gz_1'=2] {'gx_0','gx_1'}, dimensions={0} | all-to-all | bytes 6291456 | tf_op jit(solution)/shard_map/all_to_all | solution.py:100
  216.7 1.7 copy.19
  (25 shorter events, 5.3 us)
Async XLA Ops:
  3.8 18.3 %all-to-all-start = ((bf16[4,1,4,8,8,512]{5,4,3,2,1,0:T(8,128)(2,1)}), bf16[4,1,4,8,8,512]{5,4,3,2,1,0:T(8,128)(2,1)S(1)}, u32[]{:S(2)}, u32[]{:S(2)}) async-start(bf16[4,1,4,8,8,512]{5,4,3,2,1,0:T(8,128)(2,1)} %get-tuple-element.22), calls=%async_computation | async-start | bytes 2097152 | tf_op jit(solution)/shard_map/all_to_all | solution.py:26
  22.1 18.3 %all-to-all-start.3 = ((bf16[4,4,1,8,8,512]{5,4,3,1,2,0:T(8,128)(2,1)}), bf16[4,4,1,8,8,512]{5,4,3,1,2,0:T(8,128)(2,1)S(1)}, u32[]{:S(2)}, u32[]{:S(2)}) async-start(bf16[4,4,1,8,8,512]{5,4,3,1,2,0:T(8,128)(2,1)} %copy.15), calls=%async_computation.3 | async-start | bytes 2097152 | tf_op jit(solution)/shard_map/all_to_all | solution.py:26
  40.3 21.8 %all-to-all-start.6 = ((bf16[8,4,4,1,8,512]{5,4,2,1,3,0:T(8,128)(2,1)}), bf16[8,4,4,1,8,512]{5,4,2,1,3,0:T(8,128)(2,1)S(1)}, u32[]{:S(2)}, u32[]{:S(2)}) async-start(bf16[8,4,4,1,8,512]{5,4,2,1,3,0:T(8,128)(2,1)} %copy.17), calls=%async_computation.6 | async-start | bytes 2097152 | tf_op jit(solution)/shard_map/all_to_all | solution.py:26
  47.7 48.3 %copy-start.3 = (s32[24]{0:T(128)S(1)}, s32[24]{0:T(128)}, u32[]{:S(2)}) copy-start(s32[24]{0:T(128)} %param.9) | copy-start | bytes 292
  47.7 73.5 %copy-start = (f32[24,512]{1,0:T(8,128)S(1)}, f32[24,512]{1,0:T(8,128)}, u32[]{:S(2)}) copy-start(f32[24,512]{1,0:T(8,128)} %param.6) | copy-start | bytes 147460
  47.7 73.5 %copy-start.1 = (f32[24,512]{1,0:T(8,128)S(1)}, f32[24,512]{1,0:T(8,128)}, u32[]{:S(2)}) copy-start(f32[24,512]{1,0:T(8,128)} %param.8) | copy-start | bytes 147460
  47.7 73.5 %copy-start.2 = (f32[24,512]{1,0:T(8,128)S(1)}, f32[24,512]{1,0:T(8,128)}, u32[]{:S(2)}) copy-start(f32[24,512]{1,0:T(8,128)} %param.7) | copy-start | bytes 147460
  62.1 8.9 %all-to-all-start.1 = ((bf16[4,1,1,8,8,512]{5,4,3,2,1,0:T(8,128)(2,1)}), bf16[4,1,1,8,8,512]{5,4,3,2,1,0:T(8,128)(2,1)S(1)}, u32[]{:S(2)}, u32[]{:S(2)}) async-start(bf16[4,1,1,8,8,512]{5,4,3,2,1,0:T(8,128)(2,1)} %bitcast.4), calls=%async_computation.1 | async-start | bytes 524288 | tf_op jit(solution)/shard_map/all_to_all | solution.py:26
  71.0 10.8 %all-to-all-start.7 = ((bf16[4,1,4,1,8,512]{5,4,2,3,1,0:T(8,128)(2,1)}), bf16[4,1,4,1,8,512]{5,4,2,3,1,0:T(8,128)(2,1)S(1)}, u32[]{:S(2)}, u32[]{:S(2)}) async-start(bf16[4,1,4,1,8,512]{5,4,2,3,1,0:T(8,128)(2,1)} %bitcast.15), calls=%async_computation.7 | async-start | bytes 262144 | tf_op jit(solution)/shard_map/all_to_all | solution.py:26
  81.8 10.8 %all-to-all-start.4 = ((bf16[8,4,1,1,8,512]{5,4,1,3,2,0:T(8,128)(2,1)}), bf16[8,4,1,1,8,512]{5,4,1,3,2,0:T(8,128)(2,1)S(1)}, u32[]{:S(2)}, u32[]{:S(2)}) async-start(bf16[8,4,1,1,8,512]{5,4,1,3,2,0:T(8,128)(2,1)} %copy.16), calls=%async_computation.4 | async-start | bytes 524288 | tf_op jit(solution)/shard_map/all_to_all | solution.py:26
  92.6 9.9 %all-to-all-start.2 = ((bf16[8,1,1,1,8,512]{5,4,3,2,1,0:T(8,128)(2,1)}), bf16[8,1,1,1,8,512]{5,4,3,2,1,0:T(8,128)(2,1)S(1)}, u32[]{:S(2)}, u32[]{:S(2)}) async-start(bf16[8,1,1,1,8,512]{5,4,3,2,1,0:T(8,128)(2,1)} %bitcast.5), calls=%async_computation.2 | async-start | bytes 131072 | tf_op jit(solution)/shard_map/all_to_all | solution.py:26
  102.5 7.5 %all-to-all-start.8 = ((bf16[4,1,1,1,8,512]{5,4,3,2,1,0:T(8,128)(2,1)}), bf16[4,1,1,1,8,512]{5,4,3,2,1,0:T(8,128)(2,1)S(1)}, u32[]{:S(2)}, u32[]{:S(2)}) async-start(bf16[4,1,1,1,8,512]{5,4,3,2,1,0:T(8,128)(2,1)} %bitcast.16), calls=%async_computation.8 | async-start | bytes 65536 | tf_op jit(solution)/shard_map/all_to_all | solution.py:26
  110.0 11.2 %all-to-all-start.5 = ((bf16[4,1,1,1,8,512]{5,4,3,2,1,0:T(8,128)(2,1)}), bf16[4,1,1,1,8,512]{5,4,3,2,1,0:T(8,128)(2,1)S(1)}, u32[]{:S(2)}, u32[]{:S(2)}) async-start(bf16[4,1,1,1,8,512]{5,4,3,2,1,0:T(8,128)(2,1)} %bitcast.11), calls=%async_computation.5 | async-start | bytes 65536 | tf_op jit(solution)/shard_map/all_to_all | solution.py:26
